TPU v7x, 32 devices: a whole 2x2x4 slice. The times are simulated.
32 devices in a mesh: tm: 16 (over z, y, x), chan: 2 (over core).
Axes of the slice: x: 2, y: 2, z: 4, core: 2. Of those that a mesh axis runs over, the one named last changes fastest.
Arguments:
- spectrum: float32 [32, 131072], P('tm', 'chan'), may hold values from -6 to 6
- offsets: int32 [64], replicated, may hold values from 0 to 16, as said below
Outputs:
- peak: float32 [131072], P('chan')
Inputs may be any that keep to these rules, and one draw needn't show every extreme that they name: `offsets`: entries 0 and 1 are 0; entry 2L + d (drift d of the section that joins blocks of L) lies in 0 to L, and is exactly L for d = 2L - 1.
All inputs are finite; a program needn't handle non-finite values.
Results may differ from a plain program's by a relative error of at most 0.00002.
Values sent between devices are 32-bit elements; how exact they have to be, the bound alone decides.
A program may use at most 64 MiB of HBM per device.

v0:
```python
import jax
import jax.numpy as jnp
from jax import lax
from jax.sharding import PartitionSpec as P


def shifted(value, axis, by):
    size = lax.axis_size(axis)
    pairs = [(i, i + by) for i in range(size) if 0 <= i + by < size]
    return lax.ppermute(value, axis, pairs)


def from_partner(value, axis, apart):
    return lax.ppermute(value, axis, [(i, i ^ 1 << apart) for i in range(lax.axis_size(axis))])


def take_window(single, amount, span_cols):
    return lax.dynamic_slice_in_dim(single, amount, span_cols)


def combine(lower_rows, upper_ext, shifts, span_cols):
    upper_two = jnp.repeat(upper_ext, 2, axis=0)
    moved = jax.vmap(take_window, in_axes=(0, 0, None))(upper_two, shifts, span_cols)
    return jnp.repeat(lower_rows, 2, axis=0) + moved


def lookup(offsets, table_ids, wanted):
    picked = jnp.where(table_ids[None, :] == wanted[:, None], offsets[None, :], 0)
    return jnp.sum(picked, axis=1)


def local(spectrum, offsets):
    rows_dev = spectrum.shape[0]
    span_cols = spectrum.shape[1]
    tm_count = lax.axis_size("tm")
    my_index = lax.axis_index("tm")
    table_ids = jnp.arange(offsets.shape[0], dtype=jnp.int32)

    def extend(upper_rows, width):
        edge = shifted(upper_rows[:, :width], "chan", -1)
        return jnp.concatenate([upper_rows, edge], axis=1)

    sums = spectrum
    length = 1
    while length < rows_dev:
        blocks = rows_dev // (2 * length)
        paired = sums.reshape(blocks, 2, length, span_cols)
        lower_rows = paired[:, 0].reshape(blocks * length, span_cols)
        upper_rows = paired[:, 1].reshape(blocks * length, span_cols)
        shifts = jnp.tile(offsets[2 * length : 4 * length], blocks)
        sums = combine(lower_rows, extend(upper_rows, length), shifts, span_cols)
        length = length * 2
    drifts = jnp.arange(rows_dev, dtype=jnp.int32)
    half = rows_dev // 2
    for bit_pos in range(tm_count.bit_length() - 1):
        length = rows_dev * 2**bit_pos
        is_low = my_index // 2**bit_pos % 2 == 0
        outgoing = jnp.where(is_low, sums[half:], sums[:half])
        incoming = from_partner(outgoing, "tm", bit_pos)
        lower_rows = jnp.where(is_low, sums[:half], incoming)
        upper_rows = jnp.where(is_low, incoming, sums[half:])
        kept = jnp.where(is_low, drifts[:half], drifts[half:])
        drifts = jnp.stack([2 * kept, 2 * kept + 1], axis=1).reshape(rows_dev)
        shifts = lookup(offsets, table_ids, 2 * length + drifts)
        sums = combine(lower_rows, extend(upper_rows, length), shifts, span_cols)
    return lax.pmax(jnp.max(sums, axis=0), "tm")


def solution(mesh):
    placed = (P("tm", "chan"), P())
    return jax.shard_map(local, mesh=mesh, in_specs=placed, out_specs=P("chan"), check_vma=False)
```

profile of v0, /device:TPU:0, one launch (start us, length us, event | category | flops | bytes accessed | tf_op | source)
XLA Modules:
  0.0 254.1 jit_solution(881644398561882470)
XLA Ops:
  14.6 11.5 %while.5 = (s32[]{:T(128)}, f32[2,65537]{1,0:T(2,128)S(1)}, s32[2,2]{1,0:T(2,128)S(1)}, f32[2,65536]{1,0:T(2,128)S(1)}, s32[]{:T(128)}, /*index=5*/s32[]{:T(128)}) while((s32[]{:T(128)}, f32[2,65537]{1,0:T(2,128)S(1)}, s32[2,2]{1,0:T(2,128)S(1)}, f32[2,65536]{1,0:T(2,128)S(1)}, s32[]{:T(128)}, /*index=5*/s32[]{:T(128)}) %tuple.99), condition=%wide.while_cond, body=%wide.while_body.sunk | while | flops 2 | bytes 1048689 | solution.py:18
  15.3 1.8 dynamic-slice.31
  17.1 3.3 %dynamic-update-slice.15 = f32[2,65536]{1,0:T(2,128)S(1)} dynamic-update-slice(f32[2,65536]{1,0:T(2,128)S(1)} %get-tuple-element.312, f32[1,65536]{1,0:T(1,128)S(1)} %dynamic-slice.31, s32[]{:T(128)} %get-tuple-element.309, s32[]{:T(128)} %constant.80.clone.1..sunk) | dynamic-update-slice | bytes 524292 | tf_op jit(solution)/shard_map/vmap()/gather
  21.0 1.8 dynamic-slice.31
  22.8 3.3 %dynamic-update-slice.15 = f32[2,65536]{1,0:T(2,128)S(1)} dynamic-update-slice(f32[2,65536]{1,0:T(2,128)S(1)} %get-tuple-element.312, f32[1,65536]{1,0:T(1,128)S(1)} %dynamic-slice.31, s32[]{:T(128)} %get-tuple-element.309, s32[]{:T(128)} %constant.80.clone.1..sunk) | dynamic-update-slice | bytes 524292 | tf_op jit(solution)/shard_map/vmap()/gather
  26.7 3.0 %collective-permute-start.1 = (f32[1,65536]{1,0:T(1,128)S(1)}, f32[1,65536]{1,0:T(1,128)S(1)}, u32[]{:S(2)}, u32[]{:S(2)}) collective-permute-start(f32[1,65536]{1,0:T(1,128)S(1)} %broadcast_select_fusion.2), channel_id=1, source_target_pairs={{0,2},{2,0},{4,6},{6,4},{8,10},{10,8},{12,14},{14,12},{16,18},{18,... | collective-permute-start | bytes 786440 | tf_op jit(solution)/shard_map/ppermute | solution.py:14
  29.8 6.2 %collective-permute-done.1 = f32[1,65536]{1,0:T(1,128)S(1)} collective-permute-done((f32[1,65536]{1,0:T(1,128)S(1)}, f32[1,65536]{1,0:T(1,128)S(1)}, u32[]{:S(2)}, u32[]{:S(2)}) %collective-permute-start.1) | collective-permute-done | bytes 262176 | tf_op jit(solution)/shard_map/ppermute | solution.py:14
  40.6 11.6 %while.6 = (s32[]{:T(128)}, f32[2,65538]{1,0:T(2,128)S(1)}, s32[2,2]{1,0:T(2,128)S(1)}, f32[2,65536]{1,0:T(2,128)S(1)}, s32[]{:T(128)}, /*index=5*/s32[]{:T(128)}) while((s32[]{:T(128)}, f32[2,65538]{1,0:T(2,128)S(1)}, s32[2,2]{1,0:T(2,128)S(1)}, f32[2,65536]{1,0:T(2,128)S(1)}, s32[]{:T(128)}, /*index=5*/s32[]{:T(128)}) %tuple.102), condition=%wide.while_cond.1, body=%wide.while_body.1.sunk | while | flops 2 | bytes 1048689 | solution.py:18
  41.2 1.8 dynamic-slice.33
  43.1 3.3 %dynamic-update-slice.16 = f32[2,65536]{1,0:T(2,128)S(1)} dynamic-update-slice(f32[2,65536]{1,0:T(2,128)S(1)} %get-tuple-element.330, f32[1,65536]{1,0:T(1,128)S(1)} %dynamic-slice.33, s32[]{:T(128)} %get-tuple-element.327, s32[]{:T(128)} %constant.80.clone.1..sunk.1) | dynamic-update-slice | bytes 524292 | tf_op jit(solution)/shard_map/vmap()/gather
  47.0 1.8 dynamic-slice.33
  48.9 3.3 %dynamic-update-slice.16 = f32[2,65536]{1,0:T(2,128)S(1)} dynamic-update-slice(f32[2,65536]{1,0:T(2,128)S(1)} %get-tuple-element.330, f32[1,65536]{1,0:T(1,128)S(1)} %dynamic-slice.33, s32[]{:T(128)} %get-tuple-element.327, s32[]{:T(128)} %constant.80.clone.1..sunk.1) | dynamic-update-slice | bytes 524292 | tf_op jit(solution)/shard_map/vmap()/gather
  52.7 2.4 collective-permute-start.3
  55.2 6.5 %collective-permute-done.3 = f32[1,65536]{1,0:T(1,128)S(1)} collective-permute-done((f32[1,65536]{1,0:T(1,128)S(1)}, f32[1,65536]{1,0:T(1,128)S(1)}, u32[]{:S(2)}, u32[]{:S(2)}) %collective-permute-start.3) | collective-permute-done | bytes 262176 | tf_op jit(solution)/shard_map/ppermute | solution.py:14
  66.3 11.3 %while.7 = (s32[]{:T(128)}, f32[2,65540]{1,0:T(2,128)S(1)}, s32[2,2]{1,0:T(2,128)S(1)}, f32[2,65536]{1,0:T(2,128)S(1)}, s32[]{:T(128)}, /*index=5*/s32[]{:T(128)}) while((s32[]{:T(128)}, f32[2,65540]{1,0:T(2,128)S(1)}, s32[2,2]{1,0:T(2,128)S(1)}, f32[2,65536]{1,0:T(2,128)S(1)}, s32[]{:T(128)}, /*index=5*/s32[]{:T(128)}) %tuple.105), condition=%wide.while_cond.2, body=%wide.while_body.2.sunk | while | flops 2 | bytes 1048689 | solution.py:18
  68.7 3.3 %dynamic-update-slice.17 = f32[2,65536]{1,0:T(2,128)S(1)} dynamic-update-slice(f32[2,65536]{1,0:T(2,128)S(1)} %get-tuple-element.348, f32[1,65536]{1,0:T(1,128)S(1)} %dynamic-slice.35, s32[]{:T(128)} %get-tuple-element.345, s32[]{:T(128)} %constant.80.clone.1..sunk.2) | dynamic-update-slice | bytes 524292 | tf_op jit(solution)/shard_map/vmap()/gather
  74.4 3.3 %dynamic-update-slice.17 = f32[2,65536]{1,0:T(2,128)S(1)} dynamic-update-slice(f32[2,65536]{1,0:T(2,128)S(1)} %get-tuple-element.348, f32[1,65536]{1,0:T(1,128)S(1)} %dynamic-slice.35, s32[]{:T(128)} %get-tuple-element.345, s32[]{:T(128)} %constant.80.clone.1..sunk.2) | dynamic-update-slice | bytes 524292 | tf_op jit(solution)/shard_map/vmap()/gather
  78.2 1.9 collective-permute-start.5
  80.2 6.5 %collective-permute-done.5 = f32[1,65536]{1,0:T(1,128)S(1)} collective-permute-done((f32[1,65536]{1,0:T(1,128)S(1)}, f32[1,65536]{1,0:T(1,128)S(1)}, u32[]{:S(2)}, u32[]{:S(2)}) %collective-permute-start.5) | collective-permute-done | bytes 262176 | tf_op jit(solution)/shard_map/ppermute | solution.py:14
  91.3 11.3 %while.8 = (s32[]{:T(128)}, f32[2,65544]{1,0:T(2,128)S(1)}, s32[2,2]{1,0:T(2,128)S(1)}, f32[2,65536]{1,0:T(2,128)S(1)}, s32[]{:T(128)}, /*index=5*/s32[]{:T(128)}) while((s32[]{:T(128)}, f32[2,65544]{1,0:T(2,128)S(1)}, s32[2,2]{1,0:T(2,128)S(1)}, f32[2,65536]{1,0:T(2,128)S(1)}, s32[]{:T(128)}, /*index=5*/s32[]{:T(128)}) %tuple.108), condition=%wide.while_cond.3, body=%wide.while_body.3.sunk | while | flops 2 | bytes 1048689 | solution.py:18
  91.9 1.8 dynamic-slice.37
  93.7 3.3 %dynamic-update-slice.18 = f32[2,65536]{1,0:T(2,128)S(1)} dynamic-update-slice(f32[2,65536]{1,0:T(2,128)S(1)} %get-tuple-element.366, f32[1,65536]{1,0:T(1,128)S(1)} %dynamic-slice.37, s32[]{:T(128)} %get-tuple-element.363, s32[]{:T(128)} %constant.80.clone.1..sunk.3) | dynamic-update-slice | bytes 524292 | tf_op jit(solution)/shard_map/vmap()/gather
  97.5 1.8 dynamic-slice.37
  99.4 3.3 %dynamic-update-slice.18 = f32[2,65536]{1,0:T(2,128)S(1)} dynamic-update-slice(f32[2,65536]{1,0:T(2,128)S(1)} %get-tuple-element.366, f32[1,65536]{1,0:T(1,128)S(1)} %dynamic-slice.37, s32[]{:T(128)} %get-tuple-element.363, s32[]{:T(128)} %constant.80.clone.1..sunk.3) | dynamic-update-slice | bytes 524292 | tf_op jit(solution)/shard_map/vmap()/gather
  103.2 2.8 %collective-permute-start.7 = (f32[1,65536]{1,0:T(1,128)S(1)}, f32[1,65536]{1,0:T(1,128)S(1)}, u32[]{:S(2)}, u32[]{:S(2)}) collective-permute-start(f32[1,65536]{1,0:T(1,128)S(1)} %broadcast_select_fusion.11), channel_id=1, source_target_pairs={{0,16},{2,18},{4,20},{6,22},{8,24},{10,26},{12,28},{14,30},{16,0},... | collective-permute-start | bytes 786440 | tf_op jit(solution)/shard_map/ppermute | solution.py:14
  106.0 12.3 %collective-permute-done.7 = f32[1,65536]{1,0:T(1,128)S(1)} collective-permute-done((f32[1,65536]{1,0:T(1,128)S(1)}, f32[1,65536]{1,0:T(1,128)S(1)}, u32[]{:S(2)}, u32[]{:S(2)}) %collective-permute-start.7) | collective-permute-done | bytes 262176 | tf_op jit(solution)/shard_map/ppermute | solution.py:14
  122.8 11.6 %while.9 = (s32[]{:T(128)}, f32[2,65552]{1,0:T(2,128)S(1)}, s32[2,2]{1,0:T(2,128)S(1)}, f32[2,65536]{1,0:T(2,128)S(1)}, s32[]{:T(128)}, /*index=5*/s32[]{:T(128)}) while((s32[]{:T(128)}, f32[2,65552]{1,0:T(2,128)S(1)}, s32[2,2]{1,0:T(2,128)S(1)}, f32[2,65536]{1,0:T(2,128)S(1)}, s32[]{:T(128)}, /*index=5*/s32[]{:T(128)}) %tuple.111), condition=%wide.while_cond.4, body=%wide.while_body.4.sunk | while | flops 2 | bytes 1048689 | solution.py:18
  123.5 1.9 dynamic-slice.39
  125.4 3.3 %dynamic-update-slice.19 = f32[2,65536]{1,0:T(2,128)S(1)} dynamic-update-slice(f32[2,65536]{1,0:T(2,128)S(1)} %get-tuple-element.384, f32[1,65536]{1,0:T(1,128)S(1)} %dynamic-slice.39, s32[]{:T(128)} %get-tuple-element.381, s32[]{:T(128)} %constant.80.clone.1..sunk.4) | dynamic-update-slice | bytes 524292 | tf_op jit(solution)/shard_map/vmap()/gather
  129.3 1.9 dynamic-slice.39
  131.2 3.3 %dynamic-update-slice.19 = f32[2,65536]{1,0:T(2,128)S(1)} dynamic-update-slice(f32[2,65536]{1,0:T(2,128)S(1)} %get-tuple-element.384, f32[1,65536]{1,0:T(1,128)S(1)} %dynamic-slice.39, s32[]{:T(128)} %get-tuple-element.381, s32[]{:T(128)} %constant.80.clone.1..sunk.4) | dynamic-update-slice | bytes 524292 | tf_op jit(solution)/shard_map/vmap()/gather
  136.2 109.4 %all-reduce.2.cloned.1.call-done = f32[65536]{0:T(1024)} async-done(((f32[65536]{0:T(1024)}), f32[65536]{0:T(1024)}) %all-reduce.2.cloned.1.call-update) | async-done | bytes 262160 | tf_op jit(solution)/shard_map/pmax | solution.py:66
  (89 shorter events, 40.9 us)
Async XLA Ops:
  6.5 239.1 %all-reduce.2.cloned.1.call-start = ((), (), s32[]{:S(2)}) async-start(), calls=%async_computation | async-start | bytes 524288 | tf_op jit(solution)/shard_map/pmax | solution.py:66
  8.7 4.2 %collective-permute-start = (f32[1,1]{1,0:T(1,128)}, f32[1,1]{1,0:T(1,128)}, u32[]{:S(2)}, u32[]{:S(2)}) collective-permute-start(f32[1,1]{1,0:T(1,128)} %slice.144), channel_id=1, source_target_pairs={{1,0},{3,2},{5,4},{7,6},{9,8},{11,10},{13,12},{15,14},{17,16},{19,... | collective-permute-start | bytes 20 | tf_op jit(solution)/shard_map/ppermute | solution.py:10
  11.5 0.7 copy-start
  26.7 9.3 %collective-permute-start.1 = (f32[1,65536]{1,0:T(1,128)S(1)}, f32[1,65536]{1,0:T(1,128)S(1)}, u32[]{:S(2)}, u32[]{:S(2)}) collective-permute-start(f32[1,65536]{1,0:T(1,128)S(1)} %broadcast_select_fusion.2), channel_id=1, source_target_pairs={{0,2},{2,0},{4,6},{6,4},{8,10},{10,8},{12,14},{14,12},{16,18},{18,... | collective-permute-start | bytes 786440 | tf_op jit(solution)/shard_map/ppermute | solution.py:14
  36.5 3.1 %collective-permute-start.2 = (f32[1,2]{1,0:T(1,128)S(1)}, f32[1,2]{1,0:T(1,128)S(1)}, u32[]{:S(2)}, u32[]{:S(2)}) collective-permute-start(f32[1,2]{1,0:T(1,128)S(1)} %slice.147), channel_id=1, source_target_pairs={{1,0},{3,2},{5,4},{7,6},{9,8},{11,10},{13,12},{15,14},{17,16},{19,... | collective-permute-start | bytes 32 | tf_op jit(solution)/shard_map/ppermute | solution.py:10
  52.7 9.0 %collective-permute-start.3 = (f32[1,65536]{1,0:T(1,128)S(1)}, f32[1,65536]{1,0:T(1,128)S(1)}, u32[]{:S(2)}, u32[]{:S(2)}) collective-permute-start(f32[1,65536]{1,0:T(1,128)S(1)} %broadcast_select_fusion.5), channel_id=1, source_target_pairs={{0,4},{2,6},{4,0},{6,2},{8,12},{10,14},{12,8},{14,10},{16,20},{18,... | collective-permute-start | bytes 786440 | tf_op jit(solution)/shard_map/ppermute | solution.py:14
  62.2 3.1 %collective-permute-start.4 = (f32[1,4]{1,0:T(1,128)S(1)}, f32[1,4]{1,0:T(1,128)S(1)}, u32[]{:S(2)}, u32[]{:S(2)}) collective-permute-start(f32[1,4]{1,0:T(1,128)S(1)} %slice.150), channel_id=1, source_target_pairs={{1,0},{3,2},{5,4},{7,6},{9,8},{11,10},{13,12},{15,14},{17,16},{19,... | collective-permute-start | bytes 56 | tf_op jit(solution)/shard_map/ppermute | solution.py:10
  78.2 8.5 %collective-permute-start.5 = (f32[1,65536]{1,0:T(1,128)S(1)}, f32[1,65536]{1,0:T(1,128)S(1)}, u32[]{:S(2)}, u32[]{:S(2)}) collective-permute-start(f32[1,65536]{1,0:T(1,128)S(1)} %broadcast_select_fusion.8), channel_id=1, source_target_pairs={{0,8},{2,10},{4,12},{6,14},{8,0},{10,2},{12,4},{14,6},{16,24},{18,... | collective-permute-start | bytes 786440 | tf_op jit(solution)/shard_map/ppermute | solution.py:14
  87.2 3.1 %collective-permute-start.6 = (f32[1,8]{1,0:T(1,128)S(1)}, f32[1,8]{1,0:T(1,128)S(1)}, u32[]{:S(2)}, u32[]{:S(2)}) collective-permute-start(f32[1,8]{1,0:T(1,128)S(1)} %slice.153), channel_id=1, source_target_pairs={{1,0},{3,2},{5,4},{7,6},{9,8},{11,10},{13,12},{15,14},{17,16},{19,... | collective-permute-start | bytes 104 | tf_op jit(solution)/shard_map/ppermute | solution.py:10
  103.2 15.1 %collective-permute-start.7 = (f32[1,65536]{1,0:T(1,128)S(1)}, f32[1,65536]{1,0:T(1,128)S(1)}, u32[]{:S(2)}, u32[]{:S(2)}) collective-permute-start(f32[1,65536]{1,0:T(1,128)S(1)} %broadcast_select_fusion.11), channel_id=1, source_target_pairs={{0,16},{2,18},{4,20},{6,22},{8,24},{10,26},{12,28},{14,30},{16,0},... | collective-permute-start | bytes 786440 | tf_op jit(solution)/shard_map/ppermute | solution.py:14
  118.7 3.1 %collective-permute-start.8 = (f32[1,16]{1,0:T(1,128)S(1)}, f32[1,16]{1,0:T(1,128)S(1)}, u32[]{:S(2)}, u32[]{:S(2)}) collective-permute-start(f32[1,16]{1,0:T(1,128)S(1)} %slice.156), channel_id=1, source_target_pairs={{1,0},{3,2},{5,4},{7,6},{9,8},{11,10},{13,12},{15,14},{17,16},{19,... | collective-permute-start | bytes 200 | tf_op jit(solution)/shard_map/ppermute | solution.py:10
Sparse Core Ops, SparseCore 0:
  136.3 109.2 all-reduce.1
where the time goes:
time: 255 us; the launch traced here: 254 us
  waiting for transfers between devices  148 us (58%)
  local copies, waits for them, and re-layouts  64.3 us (25%)
  starting transfers between devices  16.7 us (7%)
  between operations  14.6 us (6%)
  other arithmetic  10.4 us (4%)
    pmax x1, waiting for transfers between devices, local(): return lax.pmax(jnp.max(sums, axis=0), 'tm')  109 us
    gather x40, local copies, waits for them, and re-layouts  57 us
    ppermute x4, waiting for transfers between devices, from_partner(): lax.ppermute(value, axis, [(i, i ^ 1 << apart) for i in range(lax.axis_si...  31.6 us
    ppermute x4, starting transfers between devices, from_partner(): lax.ppermute(value, axis, [(i, i ^ 1 << apart) for i in range(lax.axis_si...  10.1 us
    ppermute x5, waiting for transfers between devices, shifted(): return lax.ppermute(value, axis, pairs)  6.75 us
    ppermute x5, starting transfers between devices, shifted(): return lax.ppermute(value, axis, pairs)  6.63 us
  transfers between devices with their start and end apart: 10, of which 9 were waited for; matrix products, arithmetic and copies ran while one was open for 1% of the time, Pallas kernels for 0%

commit v1 on v0

v1 whole, which is shorter than its diff:
```python
import functools

import jax
import jax.numpy as jnp
from jax import lax
from jax.experimental import pallas as pl
from jax.experimental.pallas import tpu as pltpu
from jax.sharding import PartitionSpec as P

LANES = 128
MESH = pl.DeviceIdType.MESH


def round_up(value, to):
    return (value + to - 1) // to * to


def flip(place, bits):
    out, bit = place, 1
    while bit <= bits:
        if bits & bit:
            out = out + bit * (1 - 2 * lax.rem(lax.div(place, bit), 2))
        bit *= 2
    return out


def kernel(count, chans, rows, tiles, halo, offs_ref, x_ref, out_ref, recv, *rest):
    levels = rest[:-5]
    send_sem, recv_sem, edge_sem, send_sem2, recv_sem2 = rest[-5:]
    me = lax.axis_index("tm")
    col = lax.axis_index("chan")
    total = count * rows
    body = tiles
    full = tiles + halo
    at_end = me == count - 1
    no_next = me * chans + col == count * chans - 1

    barrier = pltpu.get_barrier_semaphore()
    for j in range(1, count):
        pl.semaphore_signal(barrier, inc=1, device_id=(flip(me, j), col), device_id_type=MESH)
    if chans > 1:
        @pl.when(jnp.logical_and(at_end, col < chans - 1))
        def _():
            for t in range(count):
                pl.semaphore_signal(barrier, inc=1, device_id=(t, jnp.minimum(col + 1, chans - 1)), device_id_type=MESH)
    pl.semaphore_wait(barrier, count - 1 + jnp.where(col > 0, 1, 0))

    def to_peer(j, size):
        k = flip(me, j)
        return pltpu.make_async_remote_copy(
            src_ref=x_ref.at[pl.ds(k * body, size)],
            dst_ref=recv.at[me, pl.ds(0, size)],
            send_sem=send_sem.at[j],
            recv_sem=recv_sem.at[me],
            device_id=(k, col),
            device_id_type=MESH,
        )

    def both(j, act):
        @pl.when(flip(me, j) == count - 1)
        def _():
            act(to_peer(j, body))

        @pl.when(flip(me, j) != count - 1)
        def _():
            act(to_peer(j, full))

    def edge():
        return pltpu.make_async_remote_copy(
            src_ref=x_ref.at[pl.ds(0, halo)],
            dst_ref=recv.at[me, pl.ds(body, halo)],
            send_sem=edge_sem.at[0],
            recv_sem=recv_sem.at[me],
            device_id=(count - 1, jnp.maximum(col - 1, 0)),
            device_id_type=MESH,
        )

    def own(size):
        return pltpu.make_async_copy(
            x_ref.at[pl.ds(me * body, size)], recv.at[me, pl.ds(0, size)], recv_sem.at[me]
        )

    for j in reversed(range(1, count)):
        both(j, lambda copy: copy.start())
    if chans > 1:
        @pl.when(col > 0)
        def _():
            edge().start()

    @pl.when(at_end)
    def _():
        own(body).start()

    @pl.when(me != count - 1)
    def _():
        own(full).start()

    @pl.when(no_next)
    def _():
        for t in range(count):
            recv[t, pl.ds(body, halo)] = jnp.zeros((halo, rows, LANES), jnp.float32)

    def arrived(t):
        def wait(size):
            part = recv.at[t, pl.ds(0, size)]
            pltpu.make_async_copy(part, part, recv_sem.at[t]).wait()

        @pl.when(no_next)
        def _():
            wait(body)

        @pl.when(me * chans + col != count * chans - 1)
        def _():
            wait(full)

    def node(length, block, slot=0, inner=0):
        at = length.bit_length() - 1
        wide = tiles + (total - 2 * length + LANES - 1) // LANES
        lane = lax.broadcasted_iota(jnp.int32, (wide, LANES), 1)

        def load(which, d, start):
            if length == 1:
                return recv[slot, pl.ds(start, wide), 2 * inner + which]
            return levels[at - 1][2 * block + which, d, pl.ds(start, wide)]

        peak = None
        for half in range(length):
            low = load(0, half, 0)
            here = load(1, half, 0)
            ahead = load(1, half, 1)
            for d in (2 * half, 2 * half + 1):
                by = offs_ref[2 * length + d]
                mixed = jnp.where(lane >= by, here, ahead)
                value = low + pltpu.roll(mixed, lax.rem(LANES - by, LANES), 1)
                if 2 * length < total:
                    levels[at][block, d, pl.ds(0, wide)] = value
                else:
                    peak = value if peak is None else jnp.maximum(peak, value)
        return peak

    peak = None
    for j in range(count):
        slot = flip(me, j)
        arrived(slot)
        length = 1
        while length < rows:
            for inner in range(rows // (2 * length)):
                peak = node(length, slot * (rows // (2 * length)) + inner, slot, inner)
            length *= 2
        step = 1
        while step < count and (j + 1) % (2 * step) == 0:
            peak = node(step * rows, flip(lax.div(me, 2 * step), j // (2 * step)))
            step *= 2

    mine = pl.ds(me * tiles, tiles)
    out_ref[mine] = peak
    for j in range(1, count):
        both(j, lambda copy: copy.wait_send())
    if chans > 1:
        @pl.when(col > 0)
        def _():
            edge().wait_send()

    def result(j, t):
        part = out_ref.at[pl.ds(t * tiles, tiles)]
        return pltpu.make_async_remote_copy(
            src_ref=part,
            dst_ref=part,
            send_sem=send_sem2.at[j],
            recv_sem=recv_sem2.at[t],
            device_id=(flip(me, j), col),
            device_id_type=MESH,
        )

    for j in reversed(range(1, count)):
        result(j, me).start()
    for j in range(1, count):
        result(j, flip(me, j)).wait_recv()
    for j in range(1, count):
        result(j, me).wait_send()


def local(count, chans, spectrum, offsets):
    rows, span = spectrum.shape
    total = count * rows
    tiles = span // LANES // count
    halo = (total - 1 + LANES - 1) // LANES
    x = spectrum.reshape(rows, span // LANES, LANES).transpose(1, 0, 2)
    deep = round_up(tiles + halo, 8) + 8
    scratch = [pltpu.VMEM((count, deep, rows, LANES), jnp.float32)]
    length = 2
    while length < total:
        scratch.append(pltpu.VMEM((total // length, length, deep, LANES), jnp.float32))
        length *= 2
    dma = pltpu.SemaphoreType.DMA
    scratch += [dma((count,)), dma((count,)), dma((1,)), dma((count,)), dma((count,))]
    peak = pl.pallas_call(
        functools.partial(kernel, count, chans, rows, tiles, halo),
        out_shape=jax.ShapeDtypeStruct((count * tiles, LANES), jnp.float32),
        in_specs=[pl.BlockSpec(memory_space=pltpu.SMEM), pl.BlockSpec(memory_space=pl.ANY)],
        out_specs=pl.BlockSpec(memory_space=pltpu.VMEM),
        scratch_shapes=scratch,
        compiler_params=pltpu.CompilerParams(collective_id=0, has_side_effects=True),
    )(offsets, x)
    return peak.reshape(span)


def solution(mesh):
    body = functools.partial(local, mesh.shape["tm"], mesh.shape["chan"])
    placed = (P("tm", "chan"), P())
    return jax.shard_map(body, mesh=mesh, in_specs=placed, out_specs=P("chan"), check_vma=False)
```

time: 255 us -> 31.3 us (0.12)
  waiting for transfers between devices: 148 us -> 0 us
  local copies, waits for them, and re-layouts: 64.3 us -> 1.67 us
  Pallas kernels: 0 us -> 29.4 us
  starting transfers between devices: 16.7 us -> 0 us
  between operations: 14.6 us -> 0.01 us
  other arithmetic: 10.4 us -> 0 us
    pmax x1 -> x0, waiting for transfers between devices: 109 us -> none  [local(): return lax.pmax(jnp.max(sums, axis=0), 'tm')]
    gather x40 -> x0, local copies, waits for them, and re-layouts: 57 us -> none
    ppermute x9 -> x0, waiting for transfers between devices: 38.3 us -> none  [the longest x4 31.6 us: from_partner(): lax.ppermute(value, axis, [(i, i ^ 1 << apart) for i in range(lax.axis_si...]
    pallas_call x0 -> x1, Pallas kernels: none -> 29.4 us  [local(): pl.pallas_call(functools.partial(kernel, count, chans, rows, tiles, halo)...]
    ppermute x9 -> x0, starting transfers between devices: 16.7 us -> none  [the longest x4 10.1 us: from_partner(): lax.ppermute(value, axis, [(i, i ^ 1 << apart) for i in range(lax.axis_si...]
    concatenate x5 -> x0, other arithmetic: 4.14 us -> none  [extend(): return jnp.concatenate([upper_rows, edge], axis=1)]
    select_n x10 -> x0, other arithmetic: 2.91 us -> none  [the longest x4 1.8 us: local(): lower_rows = jnp.where(is_low, sums[:half], incoming)]
    slice x7 -> x0, local copies, waits for them, and re-layouts: 2.86 us -> none  [the longest x1 1.65 us: local(): lower_rows = paired[:, 0].reshape(blocks * length, span_cols)]
  transfers between devices with their start and end apart: 10 -> 0, of which waited for: 9 -> 0; matrix products, arithmetic and copies ran while one was open for 1% -> 0% of each run, Pallas kernels for 0% -> 0%
where the time goes in v1:
time: 31.3 us; the launch traced here: 31.1 us
  Pallas kernels  29.4 us (94%)
  local copies, waits for them, and re-layouts  1.67 us (5%)
    pallas_call x1, Pallas kernels, local(): pl.pallas_call(functools.partial(kernel, count, chans, rows, tiles, halo)...  29.4 us
    unnamed x1, local copies, waits for them, and re-layouts  1.67 us

profile of v1, /device:TPU:0, one launch (start us, length us, event | category | flops | bytes accessed | tf_op | source)
XLA Modules:
  0.0 31.1 jit_solution(1345158755518805752)
XLA Ops:
  0.0 29.4 %shard_map.28 = f32[512,128]{1,0:T(8,128)} custom-call(s32[64]{0:T(128)} %offs_ref.1, f32[512,2,128]{2,1,0:T(2,128)} %bitcast.5), custom_call_target="tpu_custom_call" | custom-call | tf_op jit(solution)/shard_map/pallas_call | solution.py:197
  29.4 1.7 %copy.4 = f32[65536]{0:T(1024)} copy(f32[65536]{0:T(1024)} %bitcast.4) | data formatting | bytes 524288

commit v2 on v1

--- a/solution.py
+++ b/solution.py
@@ -138,17 +138,18 @@
                     peak = value if peak is None else jnp.maximum(peak, value)
         return peak
 
-    peak = None
-    for j in range(count):
+    peak, done = None, set()
+    for j in list(range(count // 2)) + list(reversed(range(count // 2, count))):
         slot = flip(me, j)
         arrived(slot)
+        done.add(j)
         length = 1
         while length < rows:
             for inner in range(rows // (2 * length)):
                 peak = node(length, slot * (rows // (2 * length)) + inner, slot, inner)
             length *= 2
         step = 1
-        while step < count and (j + 1) % (2 * step) == 0:
+        while step < count and done.issuperset(range(j // (2 * step) * 2 * step, (j // (2 * step) + 1) * 2 * step)):
             peak = node(step * rows, flip(lax.div(me, 2 * step), j // (2 * step)))
             step *= 2
 

time: 31.3 us -> 30.7 us (0.981)
  Pallas kernels: 29.4 us -> 28.8 us
    pallas_call x1, Pallas kernels: 29.4 us -> 28.8 us  [local(): pl.pallas_call(functools.partial(kernel, count, chans, rows, tiles, halo)...]
where the time goes in v2:
time: 30.7 us; the launch traced here: 30.5 us
  Pallas kernels  28.8 us (94%)
  local copies, waits for them, and re-layouts  1.67 us (5%)
    pallas_call x1, Pallas kernels, local(): pl.pallas_call(functools.partial(kernel, count, chans, rows, tiles, halo)...  28.8 us
    unnamed x1, local copies, waits for them, and re-layouts  1.67 us

profile of v2, /device:TPU:0, one launch (start us, length us, event | category | flops | bytes accessed | tf_op | source)
XLA Modules:
  0.0 30.5 jit_solution(14863906643298139758)
XLA Ops:
  0.0 28.8 %shard_map.28 = f32[512,128]{1,0:T(8,128)} custom-call(s32[64]{0:T(128)} %offs_ref.1, f32[512,2,128]{2,1,0:T(2,128)} %bitcast.5), custom_call_target="tpu_custom_call" | custom-call | tf_op jit(solution)/shard_map/pallas_call | solution.py:198
  28.8 1.7 %copy.4 = f32[65536]{0:T(1024)} copy(f32[65536]{0:T(1024)} %bitcast.4) | data formatting | bytes 524288

commit v3 on v2

--- a/solution.py
+++ b/solution.py
@@ -80,12 +80,13 @@
             x_ref.at[pl.ds(me * body, size)], recv.at[me, pl.ds(0, size)], recv_sem.at[me]
         )
 
+    if chans > 1:
+        @pl.when(col > 0)
+        def _():
+            edge().start()
+
     for j in reversed(range(1, count)):
         both(j, lambda copy: copy.start())
-    if chans > 1:
-        @pl.when(col > 0)
-        def _():
-            edge().start()
 
     @pl.when(at_end)
     def _():

time: 30.7 us -> 30.4 us (level)
  no operation moved by 1% of the time
where the time goes in v3:
time: 30.4 us; the launch traced here: 30.2 us
  Pallas kernels  28.5 us (94%)
  local copies, waits for them, and re-layouts  1.67 us (5%)
    pallas_call x1, Pallas kernels, local(): pl.pallas_call(functools.partial(kernel, count, chans, rows, tiles, halo)...  28.5 us
    unnamed x1, local copies, waits for them, and re-layouts  1.67 us

profile of v3, /device:TPU:0, one launch (start us, length us, event | category | flops | bytes accessed | tf_op | source)
XLA Modules:
  0.0 30.2 jit_solution(5736958322554318421)
XLA Ops:
  0.0 28.5 %shard_map.28 = f32[512,128]{1,0:T(8,128)} custom-call(s32[64]{0:T(128)} %offs_ref.1, f32[512,2,128]{2,1,0:T(2,128)} %bitcast.5), custom_call_target="tpu_custom_call" | custom-call | tf_op jit(solution)/shard_map/pallas_call | solution.py:199
  28.5 1.7 %copy.4 = f32[65536]{0:T(1024)} copy(f32[65536]{0:T(1024)} %bitcast.4) | data formatting | bytes 524288
